TPU v7x, 512 devices: a 4x2x32 block of a 4x8x32 slice. The times are simulated.
512 devices in a mesh: group: 2 (over y), ctx: 32 (over z), head: 4 (over x), dec: 2 (over core).
Axes of the slice: x: 4, y: 2, z: 32, core: 2. Of those that a mesh axis runs over, the one named last changes fastest.
The devices are a block of a 4x8x32 slice.
Arguments:
- queries: bfloat16 [8192, 12288], P(('group', 'ctx'), ('head', 'dec')), parts along dimension 0, may hold values from -1100 to 1100
- latent_rows: bfloat16 [8192, 576], P(('group', 'ctx')), parts along dimension 0, may hold values from -8 to 8
- segments: int32 [8192], P('group'), parts along dimension 0, may hold values from 0 to 3, never falling along the last dimension, each value on 1 to 2048 neighbouring positions
- owners: int32 [8192, 1], P(('group', 'ctx')), parts along dimension 0, may hold values from 0 to 63; in each aligned block of 128 rows (0 to 127, 128 to 255, ...) at most 4 rows name the same one
- absorb_key: bfloat16 [64, 128, 512], P(('head', 'dec')), may hold values from -0.5 to 0.5
- absorb_value: bfloat16 [64, 512, 128], P(('head', 'dec')), may hold values from -0.25 to 0.25
Outputs:
- attended: bfloat16 [8192, 8192], P(('group', 'ctx'), ('head', 'dec')), parts along dimension 0
- kv_cache: bfloat16 [128, 32, 4, 576], P(('group', 'ctx', 'dec')), parts along dimension 0
There are 2 independent parts, one for each index of `group`. A program takes and returns all parts, laid end to end along the dimension named above; an argument that names none is the same for every part. Nothing has to cross between parts.
Inputs may be any that keep to these rules, and one draw needn't show every extreme that they name: `segments`: prompt numbers never fall along the tokens; each prompt has 1 to 2048 tokens and one has exactly 2048. `owners`: among the 128 tokens of one index of ctx no owner is named more than 4 times; some owner is named exactly 4 times in some of them; every owner is named somewhere.
All inputs are finite; a program needn't handle non-finite values.
Results may differ from a plain program's by a relative error of at most 0.0085.
Values may be sent and summed in bfloat16 or wider, within the bound.
No kernel may reach another device: no remote copies, remote signals or barrier semaphores. Data moves between devices by JAX's collectives and lax.ppermute only.
A program may use at most 128 MiB of HBM per device.

v0:
```python
import jax
import jax.numpy as jnp
from jax import lax
from jax.sharding import PartitionSpec as P

NOPE = 128
ROPE = 64
LATENT = 512
VDIM = 128


def rotate_pairs(rope_part, positions):
    half_rope = ROPE // 2
    frequency = 10000.0 ** (-jnp.arange(half_rope, dtype=jnp.float32) * 2.0 / ROPE)
    angles = positions.astype(jnp.float32)[:, None] * frequency[None, :]
    cosine = jnp.cos(angles)[:, None, :]
    sine_part = jnp.sin(angles)[:, None, :]
    first_part = rope_part[..., :half_rope]
    second = rope_part[..., half_rope:]
    return jnp.concatenate(
        [first_part * cosine - second * sine_part, first_part * sine_part + second * cosine],
        axis=-1,
    )


def ship_rows(latent_rows, owners):
    row_count = latent_rows.shape[0]
    ctx_count = lax.axis_size("ctx")
    dec_count = lax.axis_size("dec")
    core_index = lax.axis_index("dec")
    slots = max(2, 2 * row_count // (ctx_count * dec_count))
    owner_ids = owners[:, 0]
    row_order = jnp.arange(row_count, dtype=jnp.int32)
    earlier = row_order[None, :] < row_order[:, None]
    slot_rank = jnp.sum((owner_ids[:, None] == owner_ids[None, :]) & earlier, axis=1)
    target = owner_ids // dec_count * slots + slot_rank
    kept_rows = owner_ids % dec_count == core_index
    picker = (
        (jnp.arange(ctx_count * slots, dtype=jnp.int32)[:, None] == target[None, :])
        & kept_rows[None, :]
    ).astype(jnp.bfloat16)
    outgoing = jnp.dot(picker, latent_rows, preferred_element_type=jnp.float32).astype(jnp.bfloat16)
    outgoing = outgoing.reshape(ctx_count, slots, LATENT + ROPE)
    arrived = lax.all_to_all(outgoing, "ctx", split_axis=0, concat_axis=0, tiled=True)
    return arrived[None]


def on_device(queries, latent_rows, segments, owners, absorb_key, absorb_value):
    row_count = queries.shape[0]
    local_heads = absorb_key.shape[0]
    width = LATENT + ROPE
    ctx_index = lax.axis_index("ctx")
    scale = (NOPE + ROPE) ** (-0.5)
    shaped = queries.reshape(row_count, local_heads, NOPE + ROPE)
    offsets = jnp.arange(row_count, dtype=jnp.int32)
    query_pos = ctx_index * row_count + offsets
    query_seg = jnp.take(segments, query_pos)
    rotated = rotate_pairs(shaped[..., NOPE:].astype(jnp.float32), query_pos).astype(jnp.bfloat16)
    absorbed = jnp.einsum(
        "thn,hnc->thc", shaped[..., :NOPE], absorb_key, preferred_element_type=jnp.float32
    ).astype(jnp.bfloat16)
    full_query = jnp.concatenate([absorbed, rotated], axis=-1).reshape(
        row_count * local_heads, width
    )
    last_query = jnp.max(query_pos)
    lowest_seg = jnp.min(query_seg)
    highest_seg = jnp.max(query_seg)
    start_state = (
        jnp.full((row_count, local_heads), -1e30, jnp.float32),
        jnp.zeros((row_count, local_heads), jnp.float32),
        jnp.zeros((row_count, local_heads, LATENT), jnp.float32),
    )
    key_piece = lax.all_gather(latent_rows, "ctx", axis=0, tiled=True)
    count = key_piece.shape[0]
    key_pos = jnp.arange(count, dtype=jnp.int32)
    is_live = (
        (jnp.int32(0) <= last_query)
        & (segments[count - 1] >= lowest_seg)
        & (segments[0] <= highest_seg)
    )

    def update(carried):
        running_max, running_sum, running_out = carried
        scores = jnp.einsum("qw,kw->qk", full_query, key_piece, preferred_element_type=jnp.float32)
        scores = scores.reshape(row_count, local_heads, count) * scale
        allowed = (
            (key_pos[None, :] <= query_pos[:, None]) & (segments[None, :] == query_seg[:, None])
        )[:, None, :]
        masked = jnp.where(allowed, scores, -1e30)
        new_max = jnp.maximum(running_max, jnp.max(masked, axis=2))
        weights = jnp.where(allowed, jnp.exp(masked - new_max[..., None]), 0.0)
        new_sum = jnp.sum(weights, axis=2)
        mixed = jnp.dot(
            weights.astype(jnp.bfloat16).reshape(row_count * local_heads, count),
            key_piece[:, :LATENT],
            preferred_element_type=jnp.float32,
        )
        new_out = mixed.reshape(row_count, local_heads, LATENT)
        return (new_max, new_sum, new_out)

    final_state = lax.cond(is_live, update, lambda carried: carried, start_state)
    running_max, running_sum, running_out = final_state
    latent_out = (running_out / running_sum[..., None]).astype(jnp.bfloat16)
    answer = jnp.einsum(
        "thc,hcv->thv", latent_out, absorb_value, preferred_element_type=jnp.float32
    ).astype(jnp.bfloat16)
    answer = answer.reshape(row_count, local_heads * VDIM)
    kv_cache = ship_rows(latent_rows, owners)
    return (answer, kv_cache)


def solution(mesh):
    in_specs = (
        P(("group", "ctx"), ("head", "dec")),
        P(("group", "ctx"), None),
        P("group"),
        P(("group", "ctx"), None),
        P(("head", "dec"), None, None),
        P(("head", "dec"), None, None),
    )
    out_specs = (P(("group", "ctx"), ("head", "dec")), P(("group", "ctx", "dec"), None, None, None))
    return jax.shard_map(
        on_device, mesh=mesh, in_specs=in_specs, out_specs=out_specs, check_vma=False
    )
```

profile of v0, /device:TPU:44, one launch (start us, length us, event | category | flops | bytes accessed | tf_op | source)
XLA Modules:
  0.0 235.0 jit_solution(2218947732454641080)
XLA Ops:
  7.2 0.0 copy-start
  7.2 0.1 all-gather.2.cloned.1.call-start
  7.3 1.8 copy.31
  9.1 0.1 all-gather.2.cloned.1.call-update
  9.1 0.9 convert_reduce_fusion
  10.0 0.7 fusion.22
  10.7 0.7 multiply_add_fusion
  11.4 1.1 convolution_convert_fusion.2
  12.5 0.2 copy.35
  12.6 0.7 reshape.219
  13.4 45.8 %all-to-all-start = ((bf16[32,4,576]{2,1,0:T(4,128)(2,1)}), bf16[32,4,576]{2,1,0:T(4,128)(2,1)S(1)}, u32[]{:S(2)}, u32[]{:S(2)}) async-start(bf16[32,4,576]{2,1,0:T(4,128)(2,1)} %reshape.219), calls=%async_computation | async-start | bytes 327680 | tf_op jit(solution)/shard_map/all_to_all | solution.py:44
  59.2 1.6 gather_fusion
  60.8 0.7 fusion.24
  61.5 1.3 fusion.27
  62.9 0.7 fusion.26
  63.6 1.2 copy.28
  67.9 0.1 multiply_cosine_fusion
  68.2 0.5 fusion.14
  68.7 1.1 pad_maximum_fusion
  69.8 24.9 %all-to-all-done = bf16[32,4,576]{2,1,0:T(4,128)(2,1)S(1)} async-done(((bf16[32,4,576]{2,1,0:T(4,128)(2,1)}), bf16[32,4,576]{2,1,0:T(4,128)(2,1)S(1)}, u32[]{:S(2)}, u32[]{:S(2)}) %all-to-all-start) | async-done | bytes 147488 | tf_op jit(solution)/shard_map/all_to_all | solution.py:44
  94.7 93.2 %all-gather.2.cloned.1.call-done = bf16[4096,576]{1,0:T(8,128)(2,1)} async-done(((bf16[128,576]{1,0:T(8,128)(2,1)}), bf16[4096,576]{1,0:T(8,128)(2,1)}) %all-gather.2.cloned.1.call-update) | async-done | bytes 4718608 | tf_op jit(solution)/shard_map/all_gather | solution.py:73
  187.9 36.4 %conditional.1 = (f32[128,8]{1,0:T(8,128)S(1)}, f32[128,8,512]{2,1,0:T(8,128)S(1)}) conditional(s32[]{:T(128)} %convert_element_type.40, () %tuple.16, (s32[4096]{0:T(1024)S(1)}, s32[128]{0:T(128)S(1)}, s32[4096]{0:T(1024)S(1)}, s32[128]{0:T(128)S(1)}, bf16[128,8,576]{0,2,1:T(8,128)(2,1)}, /*index=5*/bf16[4096,576]{1,0:T(8,128)(2,1)}) %tuple.39), branch_computations={%region_3.4_spmd, %region_4.0_spmd} | conditional | flops 9182903296 | bytes 71238728 | solution.py:101
  187.9 0.5 compare_and_fusion
  188.4 2.4 %copy.32 = bf16[128,8,576]{2,1,0:T(8,128)(2,1)S(1)} copy(bf16[128,8,576]{0,2,1:T(8,128)(2,1)} %get-tuple-element.45) | data formatting | bytes 2359296 | tf_op jit(solution)/shard_map
  190.8 13.9 %fusion = (f32[1024]{0:T(1024)S(1)}, f32[1024,4096]{1,0:T(8,128)}) fusion(pred[128,4096]{1,0:T(8,128)(4,1)S(1)} %compare_and_fusion, bf16[4096,576]{1,0:T(8,128)(2,1)} %get-tuple-element.18, bf16[128,8,576]{2,1,0:T(8,128)(2,1)S(1)} %copy.32), kind=kOutput, calls=%fused_computation.3 | convolution fusion | flops 4844420096 | bytes 23203840 | tf_op jit(solution)/shard_map/cond/branch_1_fun/qw,kw->qk/dot_general | solution.py:84
  204.7 10.4 %fusion.4 = f32[128,8,512]{2,1,0:T(8,128)S(1)} fusion(f32[1024,4096]{1,0:T(8,128)} %get-tuple-element.53, f32[1024]{0:T(1024)S(1)} %broadcast_maximum_fusion, pred[128,4096]{1,0:T(8,128)(4,1)} %copy-done.2, bf16[4096,576]{1,0:T(8,128)(2,1)} %get-tuple-element.18), kind=kOutput, calls=%fused_computation.7 | convolution fusion | flops 4315938816 | bytes 23597056 | tf_op jit(solution)/shard_map/cond/branch_1_fun/dot_general | solution.py:93
  215.1 9.1 %fusion.2 = f32[1024]{0:T(1024)S(1)} fusion(f32[1024,4096]{1,0:T(8,128)} %get-tuple-element.53, f32[1024]{0:T(1024)S(1)} %broadcast_maximum_fusion, pred[128,4096]{1,0:T(8,128)(4,1)S(1)} %copy-done.3), kind=kLoop, calls=%fused_computation.5 | loop fusion | flops 20970496 | bytes 17309696 | tf_op jit(solution)/shard_map/cond/branch_1_fun/reduce_sum | solution.py:92
  224.2 0.1 reduce_sum.18
  224.3 0.2 divide_convert_fusion
  224.5 2.2 convolution_convert_fusion.1
  226.7 0.9 copy.36
  227.5 0.7 copy.47
  (14 shorter events, 0.1 us)
Async XLA Ops:
  7.2 61.0 %copy-start = (bf16[8,128,512]{2,1,0:T(8,128)(2,1)S(1)}, bf16[8,128,512]{2,1,0:T(8,128)(2,1)}, u32[]{:S(2)}) copy-start(bf16[8,128,512]{2,1,0:T(8,128)(2,1)} %param.12) | copy-start | bytes 3145732
  7.2 180.7 %copy-start.1 = (s32[4096]{0:T(1024)S(1)}, s32[4096]{0:T(1024)}, u32[]{:S(2)}) copy-start(s32[4096]{0:T(1024)} %param.10) | copy-start | bytes 49156
  7.2 180.7 %all-gather.2.cloned.1.call-start = ((), (), s32[]{:S(2)}) async-start(), calls=%async_computation.1 | async-start | bytes 5406720 | tf_op jit(solution)/shard_map/all_gather | solution.py:73
  13.4 81.3 %all-to-all-start = ((bf16[32,4,576]{2,1,0:T(4,128)(2,1)}), bf16[32,4,576]{2,1,0:T(4,128)(2,1)S(1)}, u32[]{:S(2)}, u32[]{:S(2)}) async-start(bf16[32,4,576]{2,1,0:T(4,128)(2,1)} %reshape.219), calls=%async_computation | async-start | bytes 327680 | tf_op jit(solution)/shard_map/all_to_all | solution.py:44
  188.4 16.3 %copy-start.2 = (pred[128,4096]{1,0:T(8,128)(4,1)}, pred[128,4096]{1,0:T(8,128)(4,1)S(1)}, u32[]{:S(2)}) copy-start(pred[128,4096]{1,0:T(8,128)(4,1)S(1)} %compare_and_fusion) | copy-start | bytes 1572868 | tf_op jit(solution)/shard_map/cond
  204.7 10.4 %copy-start.3 = (pred[128,4096]{1,0:T(8,128)(4,1)S(1)}, pred[128,4096]{1,0:T(8,128)(4,1)}, u32[]{:S(2)}) copy-start(pred[128,4096]{1,0:T(8,128)(4,1)} %copy-done.2) | copy-start | bytes 1572868 | tf_op jit(solution)/shard_map/cond
Sparse Core Ops, SparseCore 0:
  10.7 177.1 all-gather.1
where the time goes:
time: 236 us; the launch traced here: 235 us
  waiting for transfers between devices  118 us (50%)
  starting transfers between devices  45.8 us (19%)
  matrix products  28.1 us (12%)
  between operations  17.3 us (7%)
  other arithmetic  14.7 us (6%)
  local copies, waits for them, and re-layouts  10.9 us (5%)
    all_gather x1, waiting for transfers between devices, on_device(): key_piece = lax.all_gather(latent_rows, 'ctx', axis=0, tiled=True)  93.2 us
    all_to_all x1, starting transfers between devices, ship_rows(): lax.all_to_all(outgoing, 'ctx', split_axis=0, concat_axis=0, tiled=True)  45.8 us
    all_to_all x1, waiting for transfers between devices, ship_rows(): lax.all_to_all(outgoing, 'ctx', split_axis=0, concat_axis=0, tiled=True)  24.9 us
    dot_general x1, matrix products, update(): jnp.einsum('qw,kw->qk', full_query, key_piece, preferred_element_type=jnp...  13.9 us
    dot_general x1, matrix products, update(): jnp.dot(weights.astype(jnp.bfloat16).reshape(row_count * local_heads, cou...  10.4 us
    reduce_sum x1, other arithmetic, update(): new_sum = jnp.sum(weights, axis=2)  9.08 us
  transfers between devices with their start and end apart: 2, of which 2 were waited for; matrix products, arithmetic and copies ran while one was open for 5% of the time, Pallas kernels for 0%

commit v1 on v0

--- a/solution.py
+++ b/solution.py
@@ -1,3 +1,4 @@
+import functools
 import jax
 import jax.numpy as jnp
 from jax import lax
@@ -7,6 +8,18 @@
 ROPE = 64
 LATENT = 512
 VDIM = 128
+
+
+def boxes_work(z, chip_axis):
+    n_all = lax.axis_size(chip_axis)
+    arrivals = [n_all if dd == 0 else 1 for dd in range(z.ndim)]
+    h_now = lax.all_to_all(
+        jnp.tile(z, arrivals), chip_axis, tiled=True, split_axis=0, concat_axis=0
+    )
+    return h_now
+
+
+solve_object = functools.partial(boxes_work, chip_axis="ctx")
 
 
 def rotate_pairs(rope_part, positions):
@@ -70,7 +83,7 @@
         jnp.zeros((row_count, local_heads), jnp.float32),
         jnp.zeros((row_count, local_heads, LATENT), jnp.float32),
     )
-    key_piece = lax.all_gather(latent_rows, "ctx", axis=0, tiled=True)
+    key_piece = solve_object(latent_rows)
     count = key_piece.shape[0]
     key_pos = jnp.arange(count, dtype=jnp.int32)
     is_live = (

time: 236 us -> 558 us (2.36)
  the two profiles are of different devices: /device:TPU:44 before, /device:TPU:96 now
where the time goes in v1:
time: 558 us; the launch traced here: 557 us
  waiting for transfers between devices  411 us (74%)
  blocking collectives  76.8 us (14%)
  matrix products  26.7 us (5%)
  local copies, waits for them, and re-layouts  17.7 us (3%)
  other arithmetic  14.7 us (3%)
  starting transfers between devices  6.5 us (1%)
    all_to_all x1, waiting for transfers between devices, boxes_work(): lax.all_to_all(jnp.tile(z, arrivals), chip_axis, tiled=True, split_axis=0...  411 us
    all_to_all x1, blocking collectives, ship_rows(): lax.all_to_all(outgoing, 'ctx', split_axis=0, concat_axis=0, tiled=True)  76.8 us
    dot_general x1, matrix products, update(): jnp.einsum('qw,kw->qk', full_query, key_piece, preferred_element_type=jnp...  14.3 us
  transfers between devices with their start and end apart: 1, of which 1 were waited for; matrix products, arithmetic and copies ran while one was open for 1% of the time, Pallas kernels for 0%

profile of v1, /device:TPU:96, one launch (start us, length us, event | category | flops | bytes accessed | tf_op | source)
XLA Modules:
  0.0 557.0 jit_solution(120054820477960833)
XLA Ops:
  0.6 0.0 copy-start
  0.6 0.8 fusion.20
  1.4 0.9 convert_reduce_fusion
  2.3 0.7 multiply_add_fusion
  3.0 1.1 convolution_convert_fusion.2
  4.1 0.2 copy.44
  4.3 0.1 reshape.227
  4.3 76.8 %all_to_all.13 = bf16[32,4,576]{2,1,0:T(4,128)(2,1)S(1)} all-to-all(bf16[32,4,576]{2,1,0:T(4,128)(2,1)S(1)} %reshape.227), channel_id=1, replica_groups=mesh['group'=2,'ctx'=32,'head'=4,'dec'=2] {'ctx'}, dimensions={0} | all-to-all | bytes 294912 | tf_op jit(solution)/shard_map/all_to_all | solution.py:57
  81.1 4.1 tile.2
  85.2 6.5 %all-to-all-start = ((bf16[32,128,576]{1,2,0:T(8,128)(2,1)}), bf16[32,128,576]{1,2,0:T(8,128)(2,1)}, u32[]{:S(2)}, u32[]{:S(2)}) async-start(bf16[32,128,576]{1,2,0:T(8,128)(2,1)} %tile.2), calls=%async_computation | async-start | bytes 9437184 | tf_op jit(solution)/shard_map/all_to_all | solution.py:16
  91.7 0.2 copy.37
  92.0 1.1 gather_fusion
  93.2 0.6 fusion.25
  93.7 0.7 fusion.24
  95.7 0.6 fusion.22
  98.2 0.1 multiply_cosine_fusion
  98.5 0.5 fusion.12
  99.0 1.1 pad_maximum_fusion
  100.1 410.7 %all-to-all-done = bf16[32,128,576]{1,2,0:T(8,128)(2,1)} async-done(((bf16[32,128,576]{1,2,0:T(8,128)(2,1)}), bf16[32,128,576]{1,2,0:T(8,128)(2,1)}, u32[]{:S(2)}, u32[]{:S(2)}) %all-to-all-start) | async-done | bytes 4718624 | tf_op jit(solution)/shard_map/all_to_all | solution.py:16
  510.7 42.4 %conditional.1 = (f32[128,8]{1,0:T(8,128)S(1)}, f32[128,8,512]{2,1,0:T(8,128)S(1)}) conditional(s32[]{:T(128)} %convert_element_type.40, () %tuple.16, (s32[4096]{0:T(1024)S(1)}, s32[128]{0:T(128)S(1)}, s32[4096]{0:T(1024)S(1)}, s32[128]{0:T(128)S(1)}, bf16[128,8,576]{0,2,1:T(8,128)(2,1)}, /*index=5*/bf16[32,128,576]{1,2,0:T(8,128)(2,1)}) %tuple.39), branch_computations={%region_3.4_spmd, %region_4.0_spmd} | conditional | flops 9182903296 | bytes 104268928 | solution.py:114
  510.7 0.5 compare_and_fusion
  511.2 0.0 copy-start.4
  511.2 7.9 %copy.41 = bf16[32,128,576]{2,1,0:T(8,128)(2,1)} copy(bf16[32,128,576]{1,2,0:T(8,128)(2,1)} %get-tuple-element.55) | data formatting | bytes 9437184 | tf_op jit(solution)/shard_map
  519.1 1.9 copy.40
  521.0 14.3 %fusion = (f32[1024]{0:T(1024)S(1)}, f32[1024,4096]{1,0:T(8,128)}) fusion(pred[128,4096]{1,0:T(8,128)(4,1)S(1)} %compare_and_fusion, bf16[4096,576]{1,0:T(8,128)(2,1)} %bitcast.48, bf16[128,8,576]{2,1,0:T(8,128)(2,1)} %copy.40), kind=kOutput, calls=%fused_computation.3 | convolution fusion | flops 4844420096 | bytes 23203840 | tf_op jit(solution)/shard_map/cond/branch_1_fun/qw,kw->qk/dot_general | solution.py:97
  535.3 8.6 %fusion.4 = f32[128,8,512]{2,1,0:T(8,128)S(1)} fusion(f32[1024,4096]{1,0:T(8,128)} %get-tuple-element.62, f32[1024]{0:T(1024)S(1)} %broadcast_maximum_fusion, pred[128,4096]{1,0:T(8,128)(4,1)} %copy-done.4, bf16[4096,576]{1,0:T(8,128)(2,1)S(1)} %bitcast.49), kind=kOutput, calls=%fused_computation.7 | convolution fusion | flops 4315938816 | bytes 23597056 | tf_op jit(solution)/shard_map/cond/branch_1_fun/dot_general | solution.py:106
  543.9 9.1 %fusion.2 = f32[1024]{0:T(1024)S(1)} fusion(f32[1024,4096]{1,0:T(8,128)} %get-tuple-element.62, f32[1024]{0:T(1024)S(1)} %broadcast_maximum_fusion, pred[128,4096]{1,0:T(8,128)(4,1)S(1)} %copy-done.5), kind=kLoop, calls=%fused_computation.5 | loop fusion | flops 20970496 | bytes 17309696 | tf_op jit(solution)/shard_map/cond/branch_1_fun/reduce_sum | solution.py:105
  553.0 0.1 reduce_sum.18
  553.1 0.2 divide_convert_fusion
  553.3 2.2 convolution_convert_fusion.1
  555.5 0.9 copy.45
  556.4 0.7 copy.56
  (19 shorter events, 0.1 us)
Async XLA Ops:
  0.6 97.8 %copy-start = (bf16[8,128,512]{2,1,0:T(8,128)(2,1)S(1)}, bf16[8,128,512]{2,1,0:T(8,128)(2,1)}, u32[]{:S(2)}) copy-start(bf16[8,128,512]{2,1,0:T(8,128)(2,1)} %param.12) | copy-start | bytes 3145732
  85.2 6.5 %copy-start.6 = (bf16[128,1536]{1,0:T(8,128)(2,1)S(1)}, bf16[128,1536]{1,0:T(8,128)(2,1)}, u32[]{:S(2)}) copy-start(bf16[128,1536]{1,0:T(8,128)(2,1)} %param.8) | copy-start | bytes 1179652
  85.2 6.8 %copy-start.1 = (s32[4096]{0:T(1024)S(1)}, s32[4096]{0:T(1024)}, u32[]{:S(2)}) copy-start(s32[4096]{0:T(1024)} %param.10) | copy-start | bytes 49156
  85.2 425.5 %all-to-all-start = ((bf16[32,128,576]{1,2,0:T(8,128)(2,1)}), bf16[32,128,576]{1,2,0:T(8,128)(2,1)}, u32[]{:S(2)}, u32[]{:S(2)}) async-start(bf16[32,128,576]{1,2,0:T(8,128)(2,1)} %tile.2), calls=%async_computation | async-start | bytes 9437184 | tf_op jit(solution)/shard_map/all_to_all | solution.py:16
  510.7 8.4 %copy-start.3 = (bf16[128,8,576]{0,2,1:T(8,128)(2,1)S(1)}, bf16[128,8,576]{0,2,1:T(8,128)(2,1)}, u32[]{:S(2)}) copy-start(bf16[128,8,576]{0,2,1:T(8,128)(2,1)} %get-tuple-element.54) | copy-start | bytes 3538948 | tf_op jit(solution)/shard_map/cond
  511.2 9.8 %copy-start.4 = (pred[128,4096]{1,0:T(8,128)(4,1)}, pred[128,4096]{1,0:T(8,128)(4,1)S(1)}, u32[]{:S(2)}) copy-start(pred[128,4096]{1,0:T(8,128)(4,1)S(1)} %compare_and_fusion) | copy-start | bytes 1572868 | tf_op jit(solution)/shard_map/cond
  521.0 14.3 %copy-start.2 = (bf16[32,128,576]{2,1,0:T(8,128)(2,1)S(1)}, bf16[32,128,576]{2,1,0:T(8,128)(2,1)}, u32[]{:S(2)}) copy-start(bf16[32,128,576]{2,1,0:T(8,128)(2,1)} %copy.41) | copy-start | bytes 14155780 | tf_op jit(solution)/shard_map/cond
  535.3 8.6 %copy-start.5 = (pred[128,4096]{1,0:T(8,128)(4,1)S(1)}, pred[128,4096]{1,0:T(8,128)(4,1)}, u32[]{:S(2)}) copy-start(pred[128,4096]{1,0:T(8,128)(4,1)} %copy-done.4) | copy-start | bytes 1572868 | tf_op jit(solution)/shard_map/cond
